TPU v7x, 256 devices: a whole 4x4x8 slice. The times are simulated.
256 devices in a mesh: row: 16 (over x, y), col: 16 (over z, core).
Axes of the slice: x: 4, y: 4, z: 8, core: 2. Of those that a mesh axis runs over, the one named last changes fastest.
Arguments:
- inverse_factor: bfloat16 [8192, 8192], P('row', 'col'), may hold values from -1 to 2, as said below
- alpha_vector: float32 [8192], replicated, may hold values from -2 to 2
Outputs:
- weight_matrix: float32 [8192, 8192], P(('row', 'col'))
Inputs may be any that keep to these rules, and one draw needn't show every extreme that they name: `inverse_factor`: lower triangular: every entry above the diagonal is zero; diagonal entries lie between 1 and 2.
All inputs are finite; a program needn't handle non-finite values.
Results may differ from a plain program's by a relative error of at most 0.0003.
Values may be sent and summed in bfloat16 or wider, within the bound.
A program may use at most 64 MiB of HBM per device.

v0:
```python
import jax.numpy as jnp


def reference(inverse_factor, alpha_vector):
    gram = jnp.dot(inverse_factor.T, inverse_factor, preferred_element_type=jnp.float32)
    return gram - alpha_vector[:, None] * alpha_vector[None, :]


def solution(mesh):
    return reference
```

profile of v0, /device:TPU:25, one launch (start us, length us, event | category | flops | bytes accessed | tf_op | source)
XLA Modules:
  0.0 239.3 jit_solution(13884598741397959304)
XLA Ops:
  6.5 0.0 all-gather.3.cloned.1.call-start
  6.5 0.7 all-gather.3.cloned.1.call-update
  7.3 0.0 reduce-scatter.4.cloned.1.call-start
  7.3 60.9 %all-gather.3.cloned.1.call-done = bf16[512,8192]{1,0:T(8,128)(2,1)} async-done(((bf16[512,512]{1,0:T(8,128)(2,1)}), bf16[512,8192]{1,0:T(8,128)(2,1)}) %all-gather.3.cloned.1.call-update) | async-done | bytes 8388624 | tf_op args[0]
  68.2 13.7 %fusion = f32[8192,512]{1,0:T(8,128)} fusion(bf16[512,8192]{1,0:T(8,128)(2,1)} %all-gather.3.cloned.1.call-done, bf16[512,512]{1,0:T(8,128)(2,1)} %param), kind=kOutput, calls=%fused_computation.1 | convolution fusion | flops 4294967296 | bytes 25690112 | tf_op jit(solution)/dot_general | solution.py:5
  81.9 0.0 copy-start
  81.9 0.0 reduce-scatter.4.cloned.1.call-update
  81.9 113.6 %reduce-scatter.4.cloned.1.call-done = f32[512,512]{1,0:T(8,128)} async-done(((f32[8192,512]{1,0:T(8,128)}), f32[512,512]{1,0:T(8,128)}) %reduce-scatter.4.cloned.1.call-update) | async-done | bytes 1048592
  195.5 7.8 %all-to-all-start = ((f32[1,16,32,512]{3,2,0,1:T(8,128)}), f32[1,16,32,512]{3,2,0,1:T(8,128)S(1)}, u32[]{:S(2)}, u32[]{:S(2)}) async-start(f32[1,16,32,512]{3,2,0,1:T(8,128)} %bitcast.14), calls=%async_computation | async-start | bytes 2097152 | tf_op jit(solution)/dot_general | solution.py:5
  203.3 0.0 copy-done
  203.3 0.1 dynamic-slice.15
  203.4 27.9 %all-to-all-done = f32[1,16,32,512]{3,2,0,1:T(8,128)S(1)} async-done(((f32[1,16,32,512]{3,2,0,1:T(8,128)}), f32[1,16,32,512]{3,2,0,1:T(8,128)S(1)}, u32[]{:S(2)}, u32[]{:S(2)}) %all-to-all-start) | async-done | bytes 1048608 | tf_op jit(solution)/dot_general | solution.py:5
  231.3 0.1 copy.4
  231.3 1.1 multiply_subtract_fusion
Async XLA Ops:
  6.5 61.6 %all-gather.3.cloned.1.call-start = ((), (), s32[]{:S(2)}) async-start(), calls=%async_computation.2 | async-start | bytes 8912896 | tf_op args[0]
  7.3 188.3 %reduce-scatter.4.cloned.1.call-start = ((), (), s32[]{:S(2)}) async-start(), calls=%async_computation.3 | async-start | bytes 17825792
  81.9 121.4 %copy-start = (f32[8192]{0:T(1024)S(1)}, f32[8192]{0:T(1024)}, u32[]{:S(2)}) copy-start(f32[8192]{0:T(1024)} %param.1) | copy-start | bytes 98308
  195.5 35.7 %all-to-all-start = ((f32[1,16,32,512]{3,2,0,1:T(8,128)}), f32[1,16,32,512]{3,2,0,1:T(8,128)S(1)}, u32[]{:S(2)}, u32[]{:S(2)}) async-start(f32[1,16,32,512]{3,2,0,1:T(8,128)} %bitcast.14), calls=%async_computation | async-start | bytes 2097152 | tf_op jit(solution)/dot_general | solution.py:5
Sparse Core Ops, SparseCore 0:
  9.2 58.9 all-gather.2
  82.0 113.4 reduce-scatter.3
where the time goes:
time: 241 us; the launch traced here: 239 us
  waiting for transfers between devices  203 us (84%)
  matrix products  13.7 us (6%)
  between operations  13.4 us (6%)
  starting transfers between devices  7.79 us (3%)
    unnamed x4, waiting for transfers between devices  175 us
    dot_general x1, waiting for transfers between devices, reference(): jnp.dot(inverse_factor.T, inverse_factor, preferred_element_type=jnp.floa...  27.9 us
    dot_general x1, matrix products, reference(): jnp.dot(inverse_factor.T, inverse_factor, preferred_element_type=jnp.floa...  13.7 us
    dot_general x1, starting transfers between devices, reference(): jnp.dot(inverse_factor.T, inverse_factor, preferred_element_type=jnp.floa...  7.75 us
  transfers between devices with their start and end apart: 3, of which 3 were waited for; matrix products, arithmetic and copies ran while one was open for 0% of the time, Pallas kernels for 0%

commit v1 on v0

v1 whole, which is shorter than its diff:
```python
import functools

import jax
import jax.numpy as jnp
from jax import lax
from jax.experimental import pallas as pl
from jax.experimental.pallas import tpu as pltpu
from jax.sharding import PartitionSpec as P

MESH = pl.DeviceIdType.MESH
D = 16


def div(a, b):
    return lax.div(a, jnp.int32(b))


def rem(a, b):
    return lax.rem(a, jnp.int32(b))


def fold(c):
    return c + div(c, 8) * (15 - 2 * c)


def kernel(B, a_ref, out_ref, at, sbuf, jbuf, acc, s_send, s_recv, own_send, j_first, j_send, j_extra, j_recv, o_send, o_recv):
    T, H, R = B // D, B // 2, (B // D) * 17
    half = R // 2
    row, col = lax.axis_index("row"), lax.axis_index("col")
    x, y, core = div(row, 4), rem(row, 4), rem(col, 2)
    sign = 1 - 2 * core
    m = fold(row)

    def remote(src, dst, send, recv, r, c):
        return pltpu.make_async_remote_copy(
            src_ref=src, dst_ref=dst, send_sem=send, recv_sem=recv, device_id=(r, c), device_id_type=MESH
        )

    mirror = 15 - row
    upper = div(col, 8)
    mc = fold(col)
    j_col = row + upper * (15 - 2 * row)
    j_row = (mc, 15 - mc)
    j_slot = row + 16 * upper
    full = row >= col
    j_from = ((col, m), (15 - col, 15 - m))

    barrier = pltpu.get_barrier_semaphore()

    def greet(r, c):
        pl.semaphore_signal(barrier, inc=1, device_id=(r, c), device_id_type=MESH)

    @pl.loop(1, D)
    def _(k):
        greet(row, rem(col + k, D))
        greet(rem(row + k, D), col)

    @pl.loop(0, D)
    def _(k):
        greet(mirror, rem(col + k, D))

    for k, (r, c) in enumerate(j_from):
        valid = (col >= m) if k == 0 else (col <= m)

        @pl.when(jnp.logical_and(valid, jnp.logical_or(r != row, c != col)))
        def _(r=r, c=c):
            greet(r, c)

    at[...] = jnp.transpose(a_ref[...])
    n_full = div(row + 16 - col, 16)
    n_self = n_full * div(col + 16 - row, 16) * (1 - upper)
    pl.semaphore_wait(barrier, 46 + 2 * n_full - n_self)

    def first(h):
        return remote(
            a_ref.at[:, pl.ds(h * H, H)], jbuf.at[j_slot], j_first.at[h], j_recv.at[j_slot], j_row[h], j_col
        )

    for h in range(2):
        to_self = jnp.logical_and(j_row[h] == row, j_col == col)

        @pl.when(jnp.logical_and(full, jnp.logical_not(to_self)))
        def _(h=h):
            first(h).start()

        @pl.when(jnp.logical_and(full, to_self))
        def _(h=h):
            pltpu.make_async_copy(a_ref.at[:, pl.ds(h * H, H)], jbuf.at[j_slot], j_recv.at[j_slot]).start()

    piece = pl.multiple_of(T * col, T)
    low = sbuf.at[row, pl.ds(piece, T), :]
    high = sbuf.at[mirror, pl.ds(pl.multiple_of(T * (16 - row), T) + piece, T), :]

    @pl.when(full)
    def _():
        @pl.loop(1, D)
        def _(k):
            i = rem(col + k, D)
            src = at.at[pl.ds(pl.multiple_of(T * i, T), T), pl.ds(0, H)]
            remote(src, low, own_send, s_recv.at[0, row], row, i).start()

        pltpu.make_async_copy(at.at[pl.ds(piece, T), pl.ds(0, H)], low, s_recv.at[0, row]).start()

        @pl.loop(0, D)
        def _(k):
            i = rem(col + k, D)
            src = at.at[pl.ds(pl.multiple_of(T * i, T), T), pl.ds(H, H)]
            remote(src, high, own_send, s_recv.at[0, mirror], mirror, i).start()

    s_sent = []

    def s_row(dx, dy, sg):
        return rem(x - sg * dx + 8, 4) * 4 + rem(y - sg * dy + 8, 4)

    def s_copy(h, slot, tx, ty, sg):
        part = sbuf.at[slot, pl.ds(h * half, half), :]
        k = len(s_sent)
        c = remote(part, part, s_send.at[k], s_recv.at[h, slot], s_row(-tx, -ty, sg), col)
        c.start()
        s_sent.append(c)

    def s_wait(h, slot):
        part = sbuf.at[slot, pl.ds(h * half, half), :]
        pltpu.make_async_copy(part, part, s_recv.at[h, slot]).wait()

    def s_step(h, d1, d2):
        sg = sign if h == 0 else -sign
        at_ = (lambda p, s: (p, s)) if h == 0 else (lambda p, s: (s, p))
        slot = s_row(*at_(d1, d2), sg)
        if (d1, d2) != (0, 0):
            s_wait(h, slot)
        if d2 == 0:
            if d1 in (0, 1):
                s_copy(h, slot, *at_(1, 0), sg)
            if d1 == 0:
                s_copy(h, slot, *at_(-1, 0), sg)
            s_copy(h, slot, *at_(0, 1), sg)
            s_copy(h, slot, *at_(0, -1), sg)
        elif d2 == 1:
            s_copy(h, slot, *at_(0, 1), sg)

    j_sent, j_extras = [], []

    def j_main(t):
        ge = div(t + 16 - m, 16)
        return t * ge + (31 - t) * (1 - ge)

    def j_wait(slot):
        pltpu.make_async_copy(jbuf.at[slot], jbuf.at[slot], j_recv.at[slot]).wait()

    other = col + sign

    def j_step(t, targets):
        slot = j_main(t)
        j_wait(slot)
        base = len(j_sent)
        for n, c in enumerate(targets):
            cp = remote(jbuf.at[slot], jbuf.at[slot], j_send.at[base + n], j_recv.at[slot], row, c)
            cp.start()
            j_sent.append(cp)
        xs = 31 - m

        def extra(n, c):
            return remote(jbuf.at[xs], jbuf.at[xs], j_extra.at[base + n], j_recv.at[xs], row, c)

        @pl.when(t == m)
        def _():
            j_wait(xs)
            for n, c in enumerate(targets):
                extra(n, c).start()

        j_extras.append((t, [functools.partial(extra, n, c) for n, c in enumerate(targets)]))

    def z_at(d):
        return rem(col + 2 * sign * d + 32, D)

    s_wait_all = pltpu.make_async_copy(sbuf.at[row], sbuf.at[row], s_recv.at[0, row])
    s_wait_all.wait()
    for h in range(2):
        s_step(h, 0, 0)
    j_step(col, (z_at(1), z_at(-1), other))
    s_order = [
        [(1, 0), (-1, 0), (0, 1)],
        [(2, 0), (1, 1), (-1, 1)],
        [(2, 1)],
        [],
    ]
    for level in range(4):
        for d1, d2 in s_order[level]:
            for h in range(2):
                s_step(h, d1, d2)
        d = level + 1
        j_step(z_at(-d), ((z_at(1),) if d < 4 else ()) + (other,))
        if d < 4:
            j_step(z_at(d), ((z_at(-1),) if d < 3 else ()) + (other,))
    for d1, d2 in [(0, -1), (0, 2), (1, -1), (-1, -1), (1, 2), (-1, 2), (2, -1), (2, 2)]:
        for h in range(2):
            s_step(h, d1, d2)
    for d in range(8):
        j_step(rem(other + 2 * d, D), ())

    acc[...] = jnp.zeros_like(acc)
    for q in reversed(range(D)):
        n = T * (q + 1)
        for h in range(2):

            @pl.when((q >= m) if h == 0 else (q >= 15 - m))
            def _(q=q, n=n, h=h):
                slot = q + 16 * h
                acc[h, 0:n, :] += jnp.dot(
                    sbuf[q, 0:n, :], jbuf[slot, 0:H, :], preferred_element_type=jnp.float32
                ) + jnp.dot(
                    sbuf[15 - q, R - n : R, :], jbuf[slot, H:B, :], preferred_element_type=jnp.float32
                )

    shift = H * div(row, 8)
    starts = (pl.multiple_of(m * B + shift, H), pl.multiple_of((15 - m) * B + shift, H))
    for h in range(2):
        pltpu.make_async_copy(
            acc.at[h, pl.ds(pl.multiple_of(T * row, T), T), :], out_ref.at[:, pl.ds(starts[h], H)], o_recv
        ).start()

    @pl.loop(1, D)
    def _(k):
        r = rem(row + k, D)
        for h in range(2):
            remote(
                acc.at[h, pl.ds(pl.multiple_of(T * r, T), T), :], out_ref.at[:, pl.ds(starts[h], H)], o_send, o_recv, r, col
            ).start()

    for h in range(2):
        to_self = jnp.logical_and(j_row[h] == row, j_col == col)

        @pl.when(jnp.logical_and(full, jnp.logical_not(to_self)))
        def _(h=h):
            first(h).wait_send()

    @pl.when(full)
    def _():
        sent = at.at[pl.ds(0, T * 15 + T // 2), :]
        pltpu.make_async_copy(sent, sent, own_send).wait()

    for c in s_sent:
        c.wait_send()
    for c in j_sent:
        c.wait_send()
    for t, extras in j_extras:
        if extras:

            @pl.when(t == m)
            def _(extras=extras):
                for e in extras:
                    e().wait_send()

    done = acc.at[:, pl.ds(0, B - T), :]
    pltpu.make_async_copy(done, done, o_send).wait()
    pltpu.make_async_copy(out_ref, out_ref, o_recv).wait()


def solution(mesh):
    def body(a, alpha):
        B = a.shape[0]
        N = B * D
        T, R = B // D, (B // D) * 17
        g = pl.pallas_call(
            functools.partial(kernel, B),
            out_shape=jax.ShapeDtypeStruct((T, N), jnp.float32),
            in_specs=[pl.BlockSpec(memory_space=pltpu.VMEM)],
            out_specs=pl.BlockSpec(memory_space=pltpu.VMEM),
            scratch_shapes=[
                pltpu.VMEM((B, B), jnp.bfloat16),
                pltpu.VMEM((D, R, B // 2), jnp.bfloat16),
                pltpu.VMEM((2 * D, B, B // 2), jnp.bfloat16),
                pltpu.VMEM((2, B, B // 2), jnp.float32),
                pltpu.SemaphoreType.DMA((30,)),
                pltpu.SemaphoreType.DMA((2, D)),
                pltpu.SemaphoreType.DMA,
                pltpu.SemaphoreType.DMA((2,)),
                pltpu.SemaphoreType.DMA((16,)),
                pltpu.SemaphoreType.DMA((16,)),
                pltpu.SemaphoreType.DMA((2 * D,)),
                pltpu.SemaphoreType.DMA,
                pltpu.SemaphoreType.DMA,
            ],
            compiler_params=pltpu.CompilerParams(
                collective_id=0, has_side_effects=True, vmem_limit_bytes=40 * 1024 * 1024
            ),
        )(a)
        start = (lax.axis_index("row") * D + lax.axis_index("col")) * T
        mine = lax.dynamic_slice(alpha, (start,), (T,))
        return g - mine[:, None] * alpha[None, :]

    return jax.shard_map(
        body, mesh=mesh, in_specs=(P("row", "col"), P(None)), out_specs=P(("row", "col"), None), check_vma=False
    )
```

time: 241 us -> 125 us (0.52)
  waiting for transfers between devices: 203 us -> 0 us
  Pallas kernels: 0 us -> 122 us
  matrix products: 13.7 us -> 0 us
  between operations: 13.4 us -> 0.02 us
  starting transfers between devices: 7.79 us -> 0 us
    unnamed x4 -> x0, waiting for transfers between devices: 175 us -> none
    pallas_call x0 -> x1, Pallas kernels: none -> 122 us  [body(): pl.pallas_call(functools.partial(kernel, B), out_shape=jax.ShapeDtypeStru...]
    dot_general x1 -> x0, waiting for transfers between devices: 27.9 us -> none  [reference(): jnp.dot(inverse_factor.T, inverse_factor, preferred_element_type=jnp.floa...]
    dot_general x1 -> x0, matrix products: 13.7 us -> none  [reference(): jnp.dot(inverse_factor.T, inverse_factor, preferred_element_type=jnp.floa...]
    dot_general x1 -> x0, starting transfers between devices: 7.75 us -> none  [reference(): jnp.dot(inverse_factor.T, inverse_factor, preferred_element_type=jnp.floa...]
  transfers between devices with their start and end apart: 3 -> 0, of which waited for: 3 -> 0; matrix products, arithmetic and copies ran while one was open for 0% -> 0% of each run, Pallas kernels for 0% -> 0%
where the time goes in v1:
time: 125 us
  Pallas kernels  122 us (98%)
  local copies, waits for them, and re-layouts  1.8 us (1%)
    pallas_call x1, Pallas kernels, body(): pl.pallas_call(functools.partial(kernel, B), out_shape=jax.ShapeDtypeStru...  122 us

profile of v1, /device:TPU:25, one launch (start us, length us, event | category | flops | bytes accessed | tf_op | source)
XLA Modules:
  0.0 124.6 jit_solution(7345816344830844141)
XLA Ops:
  0.0 0.8 dynamic_slice.3
  0.8 0.0 copy-start
  0.8 1.0 copy-done
  1.8 0.0 copy-start.1
  1.8 121.7 %shard_map.28 = f32[32,8192]{1,0:T(8,128)S(1)} custom-call(bf16[512,512]{1,0:T(8,128)(2,1)S(1)} %copy-done), custom_call_target="tpu_custom_call" | custom-call | tf_op jit(solution)/shard_map/pallas_call | solution.py:265
  123.5 0.0 copy-done.1
  123.5 1.1 multiply_subtract_fusion
Async XLA Ops:
  0.8 1.0 copy-start
  1.8 121.7 %copy-start.1 = (f32[8192]{0:T(1024)S(1)}, f32[8192]{0:T(1024)}, u32[]{:S(2)}) copy-start(f32[8192]{0:T(1024)} %param.3) | copy-start | bytes 98308

commit v2 on v0

v2 whole, which is shorter than its diff:
```python
import functools

import jax
import jax.numpy as jnp
from jax import lax
from jax.experimental import pallas as pl
from jax.experimental.pallas import tpu as pltpu
from jax.sharding import PartitionSpec as P

MESH = pl.DeviceIdType.MESH
D = 16


def div(a, b):
    return lax.div(a, jnp.int32(b))


def rem(a, b):
    return lax.rem(a, jnp.int32(b))


def kernel(st, B, a_ref, out_ref, at, sbuf, jbuf, acc, swp, got, s_send, s_recv, own_send, x_send, x_recv, j_send, j_recv, o_send, o_recv):
    T, H, R = B // D, B // 2, (B // D) * 17
    Q, half = T // 2, R // 2
    row, col = lax.axis_index("row"), lax.axis_index("col")
    x, y, core = div(row, 4), rem(row, 4), rem(col, 2)
    sign = 1 - 2 * core
    mirror = 15 - row
    full = row >= col

    def rows(start, n):
        return pl.ds(pl.multiple_of(start, Q), n)

    def remote(src, dst, send, recv, r, c):
        return pltpu.make_async_remote_copy(
            src_ref=src, dst_ref=dst, send_sem=send, recv_sem=recv, device_id=(r, c), device_id_type=MESH
        )

    def wait_bytes(ref, sem):
        pltpu.make_async_copy(ref, ref, sem).wait()

    barrier = pltpu.get_barrier_semaphore()

    def greet(r, c):
        pl.semaphore_signal(barrier, inc=1, device_id=(r, c), device_id_type=MESH)

    @pl.loop(0, D)
    def _(k):
        greet(mirror, rem(col + k, D))

    @pl.loop(1, D)
    def _(k):
        greet(row, rem(col + k, D))
        greet(rem(row + k, D), col)

    at[...] = jnp.transpose(a_ref[...])
    pl.semaphore_wait(barrier, 46)

    if "f" in st:
        piece = T * col
        low = sbuf.at[row, rows(piece, T), :]
        high = sbuf.at[mirror, rows(T * (16 - row) + piece, T), :]

        @pl.when(full)
        def _():
            pltpu.make_async_copy(at.at[rows(piece, T), pl.ds(0, H)], low, s_recv.at[0, row]).start()

            @pl.loop(1, D)
            def _(k):
                i = rem(col + k, D)
                remote(at.at[rows(T * i, T), pl.ds(0, H)], low, own_send, s_recv.at[0, row], row, i).start()

            @pl.loop(0, D)
            def _(k):
                i = rem(col + k, D)
                remote(at.at[rows(T * i, T), pl.ds(H, H)], high, own_send, s_recv.at[0, mirror], mirror, i).start()

        wait_bytes(sbuf.at[row], s_recv.at[0, row])

    if "x" in st:
        here = row * T

        def pair(p):
            gx = div(row + 16 - p, 16)
            gy = div(row + 1 + p, 16)
            base = T * (row + 1)
            first = gx * (T * p) + (1 - gx) * (base + T * (15 - p) + Q)
            second = gy * (T * (15 - p) + Q) + (1 - gy) * (base + T * p)
            return first, second

        for n, start in enumerate(pair(row)):
            pltpu.make_async_copy(sbuf.at[row, rows(start, Q), :], jbuf.at[col, rows(here + Q * n, Q), :], x_recv).start()
        pltpu.make_async_copy(sbuf.at[row, pl.ds(B + Q, Q), :], jbuf.at[col, pl.ds(B, Q), :], x_recv).start()
        remote(sbuf.at[row, pl.ds(B, Q), :], jbuf.at[col, pl.ds(B + Q, Q), :], x_send, x_recv, mirror, col).start()

        @pl.loop(1, D)
        def _(k):
            p = rem(row + k, D)
            for n, start in enumerate(pair(p)):
                remote(sbuf.at[row, rows(start, Q), :], jbuf.at[col, rows(here + Q * n, Q), :], x_send, x_recv, p, col).start()

    s_sent = []

    def s_row(dx, dy, sg):
        return rem(x - sg * dx + 8, 4) * 4 + rem(y - sg * dy + 8, 4)

    def s_copy(h, slot, tx, ty, sg):
        part = sbuf.at[slot, pl.ds(h * half, half), :]
        c = remote(part, part, s_send.at[len(s_sent)], s_recv.at[h, slot], s_row(-tx, -ty, sg), col)
        c.start()
        s_sent.append(c)

    def s_step(h, d1, d2):
        if "s" not in st:
            return
        sg = sign if h == 0 else -sign
        turn = (lambda p, s: (p, s)) if h == 0 else (lambda p, s: (s, p))
        slot = s_row(*turn(d1, d2), sg)
        if (d1, d2) != (0, 0):
            wait_bytes(sbuf.at[slot, pl.ds(h * half, half), :], s_recv.at[h, slot])
        if d2 == 0:
            if d1 in (0, 1):
                s_copy(h, slot, *turn(1, 0), sg)
            if d1 == 0:
                s_copy(h, slot, *turn(-1, 0), sg)
            s_copy(h, slot, *turn(0, 1), sg)
            s_copy(h, slot, *turn(0, -1), sg)
        elif d2 == 1:
            s_copy(h, slot, *turn(0, 1), sg)

    j_sent = []
    other = col + sign

    def z_at(d):
        return rem(col + 2 * sign * d + 32, D)

    def j_step(t, targets, own=False):
        if "j" not in st:
            return
        if not own:
            wait_bytes(jbuf.at[t], j_recv.at[t])
        for c in targets:
            cp = remote(jbuf.at[t], jbuf.at[t], j_send.at[len(j_sent)], j_recv.at[t], row, c)
            cp.start()
            j_sent.append(cp)

    for h in range(2):
        s_step(h, 0, 0)
    if "x" in st:
        wait_bytes(jbuf.at[col], x_recv)
    j_step(col, (z_at(1), z_at(-1), other), True)
    s_order = [
        [(1, 0), (-1, 0), (0, 1)],
        [(2, 0), (1, 1), (-1, 1)],
        [(2, 1)],
        [],
    ]
    for level in range(4):
        for d1, d2 in s_order[level]:
            for h in range(2):
                s_step(h, d1, d2)
        d = level + 1
        j_step(z_at(-d), ((z_at(1),) if d < 4 else ()) + (other,))
        if d < 4:
            j_step(z_at(d), ((z_at(-1),) if d < 3 else ()) + (other,))
    for d1, d2 in [(0, -1), (0, 2), (1, -1), (-1, -1), (1, 2), (-1, 2), (2, -1), (2, 2)]:
        for h in range(2):
            s_step(h, d1, d2)
    for d in range(8):
        j_step(rem(other + 2 * d, D), ())

    if "c" in st:
        early = rem(lax.broadcasted_iota(jnp.int32, (1, B), 1), T) < Q
        acc[...] = jnp.zeros_like(acc)
        swp[...] = jnp.zeros_like(swp)
        other_row = 15 - row
        for s in range(D):

            def add(ref, lhs, n, start, first, second, s=s):
                right = jbuf[:, start : start + T, :].reshape(B, H)
                prod = lax.dot_general(lhs, right, (((1,), (1,)), ((), ())), preferred_element_type=jnp.float32)
                keep = jnp.logical_or(jnp.logical_and(early, first), jnp.logical_and(jnp.logical_not(early), second))
                ref[0:n, :] += jnp.where(keep, prod, 0.0)

            n = T * (s + 1)

            @pl.when(jnp.logical_or(s >= row, s >= other_row))
            def _(s=s, n=n, add=add):
                add(acc, sbuf[s, 0:n, :], n, T * s, s >= row, s >= other_row)

            k = R - n

            @pl.when(jnp.logical_or(s < row, s < other_row))
            def _(s=s, n=n, k=k, add=add):
                add(swp, sbuf[s, n:R, :], k, T * s, s < row, s < other_row)

            @pl.when(jnp.logical_or(s == row, s == other_row))
            def _(s=s, n=n, k=k, add=add):
                add(swp, sbuf[s, n:R, :], k, B, s == row, s == other_row)

        acc[...] += jnp.where(early, pltpu.roll(swp[...], B - Q, 1), pltpu.roll(swp[...], Q, 1))

    if "o" in st:
        pltpu.make_async_copy(acc.at[rows(T * row, T), :], got.at[row], o_recv).start()

        @pl.loop(1, D)
        def _(k):
            r = rem(row + k, D)
            remote(acc.at[rows(T * r, T), :], got.at[row], o_send, o_recv, r, col).start()

    if "f" in st:

        @pl.when(full)
        def _():
            wait_bytes(at.at[pl.ds(0, T * 15 + T // 2), :], own_send)

    if "x" in st:
        wait_bytes(sbuf.at[row, pl.ds(0, B - Q), :], x_send)
    for c in s_sent + j_sent:
        c.wait_send()
    if "o" in st:
        wait_bytes(acc.at[pl.ds(0, B - T), :], o_send)
        wait_bytes(got, o_recv)
    early = rem(lax.broadcasted_iota(jnp.int32, (1, B), 1), T) < Q
    for b in range(D):
        out_ref[:, B * b : B * (b + 1)] = jnp.where(early, got[b], got[15 - b])


def solution(mesh, st="fxsjco"):
    def body(a, alpha):
        B = a.shape[0]
        T, R = B // D, (B // D) * 17
        g = pl.pallas_call(
            functools.partial(kernel, st, B),
            out_shape=jax.ShapeDtypeStruct((T, B * D), jnp.float32),
            in_specs=[pl.BlockSpec(memory_space=pltpu.VMEM)],
            out_specs=pl.BlockSpec(memory_space=pltpu.VMEM),
            scratch_shapes=[
                pltpu.VMEM((B, B), jnp.bfloat16),
                pltpu.VMEM((D, R, B // 2), jnp.bfloat16),
                pltpu.VMEM((D, R, B // 2), jnp.bfloat16),
                pltpu.VMEM((B, B), jnp.float32),
                pltpu.VMEM((B, B), jnp.float32),
                pltpu.VMEM((D, T, B), jnp.float32),
                pltpu.SemaphoreType.DMA((30,)),
                pltpu.SemaphoreType.DMA((2, D)),
                pltpu.SemaphoreType.DMA,
                pltpu.SemaphoreType.DMA,
                pltpu.SemaphoreType.DMA,
                pltpu.SemaphoreType.DMA((15,)),
                pltpu.SemaphoreType.DMA((D,)),
                pltpu.SemaphoreType.DMA,
                pltpu.SemaphoreType.DMA,
            ],
            compiler_params=pltpu.CompilerParams(
                collective_id=0, has_side_effects=True, vmem_limit_bytes=40 * 1024 * 1024
            ),
        )(a)
        start = (lax.axis_index("row") * D + lax.axis_index("col")) * T
        mine = lax.dynamic_slice(alpha, (start,), (T,))
        return g - mine[:, None] * alpha[None, :]

    return jax.shard_map(
        body, mesh=mesh, in_specs=(P("row", "col"), P(None)), out_specs=P(("row", "col"), None), check_vma=False
    )
```

time: 241 us -> 91.4 us (0.38)
  waiting for transfers between devices: 203 us -> 0 us
  Pallas kernels: 0 us -> 88.3 us
  matrix products: 13.7 us -> 0 us
  between operations: 13.4 us -> 0.02 us
  starting transfers between devices: 7.79 us -> 0 us
    unnamed x4 -> x0, waiting for transfers between devices: 175 us -> none
    pallas_call x0 -> x1, Pallas kernels: none -> 88.3 us  [body(): pl.pallas_call(functools.partial(kernel, st, B), out_shape=jax.ShapeDtype...]
    dot_general x1 -> x0, waiting for transfers between devices: 27.9 us -> none  [reference(): jnp.dot(inverse_factor.T, inverse_factor, preferred_element_type=jnp.floa...]
    dot_general x1 -> x0, matrix products: 13.7 us -> none  [reference(): jnp.dot(inverse_factor.T, inverse_factor, preferred_element_type=jnp.floa...]
    dot_general x1 -> x0, starting transfers between devices: 7.75 us -> none  [reference(): jnp.dot(inverse_factor.T, inverse_factor, preferred_element_type=jnp.floa...]
  transfers between devices with their start and end apart: 3 -> 0, of which waited for: 3 -> 0; matrix products, arithmetic and copies ran while one was open for 0% -> 0% of each run, Pallas kernels for 0% -> 0%
where the time goes in v2:
time: 91.4 us; the launch traced here: 91.2 us
  Pallas kernels  88.3 us (97%)
  local copies, waits for them, and re-layouts  1.8 us (2%)
  other arithmetic  1.12 us (1%)
    pallas_call x1, Pallas kernels, body(): pl.pallas_call(functools.partial(kernel, st, B), out_shape=jax.ShapeDtype...  88.3 us

profile of v2, /device:TPU:25, one launch (start us, length us, event | category | flops | bytes accessed | tf_op | source)
XLA Modules:
  0.0 91.2 jit_solution(2475556031383550853)
XLA Ops:
  0.0 0.8 dynamic_slice.3
  0.8 0.0 copy-start
  0.8 1.0 %copy-done = bf16[512,512]{1,0:T(8,128)(2,1)S(1)} copy-done((bf16[512,512]{1,0:T(8,128)(2,1)S(1)}, bf16[512,512]{1,0:T(8,128)(2,1)}, u32[]{:S(2)}) %copy-start) | copy-done | bytes 524312
  1.8 0.0 copy-start.1
  1.8 88.3 %shard_map.28 = f32[32,8192]{1,0:T(8,128)S(1)} custom-call(bf16[512,512]{1,0:T(8,128)(2,1)S(1)} %copy-done), custom_call_target="tpu_custom_call" | custom-call | tf_op jit(solution)/shard_map/pallas_call | solution.py:233
  90.1 0.0 copy-done.1
  90.1 1.1 %multiply_subtract_fusion = f32[32,8192]{1,0:T(8,128)} fusion(f32[32,8192]{1,0:T(8,128)S(1)} %shard_map.28, f32[8192]{0:T(1024)S(1)} %copy-done.1, f32[32]{0:T(128)S(1)} %dynamic_slice.3), kind=kLoop, calls=%fused_computation | loop fusion | flops 524288 | bytes 2130048 | tf_op jit(solution)/shard_map/sub | solution.py:261
Async XLA Ops:
  0.8 1.0 %copy-start = (bf16[512,512]{1,0:T(8,128)(2,1)S(1)}, bf16[512,512]{1,0:T(8,128)(2,1)}, u32[]{:S(2)}) copy-start(bf16[512,512]{1,0:T(8,128)(2,1)} %a_ref.1) | copy-start | bytes 1572868
  1.8 88.3 %copy-start.1 = (f32[8192]{0:T(1024)S(1)}, f32[8192]{0:T(1024)}, u32[]{:S(2)}) copy-start(f32[8192]{0:T(1024)} %param.3) | copy-start | bytes 98308

commit v3 on v2

v3 whole, which is shorter than its diff:
```python
import functools

import jax
import jax.numpy as jnp
from jax import lax
from jax.experimental import pallas as pl
from jax.experimental.pallas import tpu as pltpu
from jax.sharding import PartitionSpec as P

MESH = pl.DeviceIdType.MESH
D = 16
SUB = 2
VM = 40 * 1024 * 1024


def div(a, b):
    return lax.div(a, jnp.int32(b))


def rem(a, b):
    return lax.rem(a, jnp.int32(b))


def kernel(
    st,
    B,
    a_hbm,
    alpha_ref,
    out_ref,
    a_ref,
    at,
    sbuf,
    jbuf,
    acc,
    got,
    a_sem,
    s_send,
    s_recv,
    own_send,
    x_send,
    x_recv,
    j_send,
    j_recv,
    o_send,
    o_recv,
):
    T, H, R = B // D, B // 2, (B // D) * 17
    Q, half, sub = T // 2, R // 2, R // SUB
    row, col = lax.axis_index("row"), lax.axis_index("col")
    x, y, core = div(row, 4), rem(row, 4), rem(col, 2)
    sign = 1 - 2 * core
    mirror = 15 - row
    full = row >= col

    def rows(start, n):
        return pl.ds(pl.multiple_of(start, Q), n)

    def remote(src, dst, send, recv, r, c):
        return pltpu.make_async_remote_copy(
            src_ref=src, dst_ref=dst, send_sem=send, recv_sem=recv, device_id=(r, c), device_id_type=MESH
        )

    def wait_bytes(ref, sem):
        pltpu.make_async_copy(ref, ref, sem).wait()

    barrier = pltpu.get_barrier_semaphore()

    def greet(r, c):
        pl.semaphore_signal(barrier, inc=1, device_id=(r, c), device_id_type=MESH)

    load = pltpu.make_async_copy(a_hbm, a_ref, a_sem)
    load.start()

    @pl.loop(0, D)
    def _(k):
        greet(mirror, rem(col + k, D))

    @pl.loop(1, D)
    def _(k):
        greet(row, rem(col + k, D))
        greet(rem(row + k, D), col)

    load.wait()
    at[...] = jnp.transpose(a_ref[...])
    pl.semaphore_wait(barrier, 46)

    def far_first(k):
        return rem(col + 24 + (1 - 2 * rem(k, 2)) * div(k + 1, 2), D)

    if "f" in st:
        piece = T * col
        low = sbuf.at[row, rows(piece, T), :]
        high = sbuf.at[mirror, rows(T * (16 - row) + piece, T), :]

        @pl.when(full)
        def _():
            @pl.loop(0, D)
            def _(k):
                i = far_first(k)
                remote(at.at[rows(T * i, T), pl.ds(H, H)], high, own_send, s_recv.at[0, mirror], mirror, i).start()

            @pl.loop(0, D - 1)
            def _(k):
                i = far_first(k)
                remote(at.at[rows(T * i, T), pl.ds(0, H)], low, own_send, s_recv.at[0, row], row, i).start()

            pltpu.make_async_copy(at.at[rows(piece, T), pl.ds(0, H)], low, s_recv.at[0, row]).start()

        wait_bytes(sbuf.at[row], s_recv.at[0, row])

    if "x" in st:
        here = row * T

        def pair(p):
            gx = div(row + 16 - p, 16)
            gy = div(row + 1 + p, 16)
            base = T * (row + 1)
            first = gx * (T * p) + (1 - gx) * (base + T * (15 - p) + Q)
            second = gy * (T * (15 - p) + Q) + (1 - gy) * (base + T * p)
            return first, second

        @pl.loop(1, D)
        def _(k):
            p = rem(row + k, D)
            for n, start in enumerate(pair(p)):
                remote(sbuf.at[row, rows(start, Q), :], jbuf.at[col, rows(here + Q * n, Q), :], x_send, x_recv, p, col).start()

        remote(sbuf.at[row, pl.ds(B, Q), :], jbuf.at[col, pl.ds(B + Q, Q), :], x_send, x_recv, mirror, col).start()
        for n, start in enumerate(pair(row)):
            pltpu.make_async_copy(sbuf.at[row, rows(start, Q), :], jbuf.at[col, rows(here + Q * n, Q), :], x_recv).start()
        pltpu.make_async_copy(sbuf.at[row, pl.ds(B + Q, Q), :], jbuf.at[col, pl.ds(B, Q), :], x_recv).start()

    s_sent = []

    def s_row(dx, dy, sg):
        return rem(x - sg * dx + 8, 4) * 4 + rem(y - sg * dy + 8, 4)

    def s_copy(h, slot, tx, ty, sg):
        part = sbuf.at[slot, pl.ds(h * half, half), :]
        c = remote(part, part, s_send.at[len(s_sent)], s_recv.at[h, slot], s_row(-tx, -ty, sg), col)
        c.start()
        s_sent.append(c)

    def s_step(d1, d2):
        if "s" not in st:
            return
        for h in range(2):
            sg = sign if h == 0 else -sign
            turn = (lambda p, s: (p, s)) if h == 0 else (lambda p, s: (s, p))
            slot = s_row(*turn(d1, d2), sg)
            if (d1, d2) != (0, 0):
                wait_bytes(sbuf.at[slot, pl.ds(h * half, half), :], s_recv.at[h, slot])
            if d2 == 0:
                if d1 in (0, 1):
                    s_copy(h, slot, *turn(1, 0), sg)
                if d1 == 0:
                    s_copy(h, slot, *turn(-1, 0), sg)
                s_copy(h, slot, *turn(0, 1), sg)
                s_copy(h, slot, *turn(0, -1), sg)
            elif d2 == 1:
                s_copy(h, slot, *turn(0, 1), sg)

    j_sent = []
    other = col + sign

    def z_at(d):
        return rem(col + 2 * sign * d + 32, D)

    def j_pass(t, u, targets, own=False):
        if "j" not in st:
            return
        part = jbuf.at[t, pl.ds(u * sub, sub), :]
        if not own:
            wait_bytes(part, j_recv.at[t, u])
        for c in targets:
            cp = remote(part, part, j_send.at[len(j_sent)], j_recv.at[t, u], row, c)
            cp.start()
            j_sent.append(cp)

    def j_step(d, u):
        j_pass(z_at(-d), u, ((z_at(1),) if d < 4 else ()) + (other,))
        if d < 4:
            j_pass(z_at(d), u, ((z_at(-1),) if d < 3 else ()) + (other,))

    s_step(0, 0)
    if "x" in st:
        wait_bytes(jbuf.at[col], x_recv)
    for u in range(SUB):
        j_pass(col, u, (z_at(1), z_at(-1)), True)
    for u in range(SUB):
        j_pass(col, u, (other,), True)
    when = [(5.0, s_step, (1, 0)), (5.1, s_step, (-1, 0)), (8.0, s_step, (0, 1)), (9.5, s_step, (2, 0)),
            (12.5, s_step, (1, 1)), (12.6, s_step, (-1, 1)), (17.0, s_step, (2, 1))]
    for d in range(1, 5):
        for u in range(SUB):
            when.append((4 + 5 * d + 6 / SUB * u, j_step, (d, u)))
    for _, step, args in sorted(when, key=lambda e: e[0]):
        step(*args)
    for d1, d2 in [(0, -1), (0, 2), (1, -1), (-1, -1), (1, 2), (-1, 2), (2, -1), (2, 2)]:
        s_step(d1, d2)
    for d in range(8):
        for u in range(SUB):
            j_pass(rem(other + 2 * d, D), u, ())

    def right(start):
        return jbuf[:, start, :].reshape(H, H)

    def times(lhs, rhs):
        return lax.dot_general(lhs, rhs, (((1,), (1,)), ((), ())), preferred_element_type=jnp.float32)

    for g in range(2):
        first_block = mirror if g else row
        if "c" in st:
            acc[g] = jnp.zeros_like(acc[g])
            for q in range(D):
                n = T * (q + 1)

                @pl.when(q >= first_block)
                def _(q=q, n=n, g=g):
                    at_end = 1 - div(q - first_block + 15, 16)
                    start = (1 - at_end) * (T * (15 - q) + Q * (1 - g)) + at_end * (B + Q * (1 - g))
                    acc[g, 0:n, :] += times(sbuf[q, 0:n, :], right(pl.ds(T * q + Q * g, Q))) + times(
                        sbuf[15 - q, R - n : R, :], right(rows(start, Q))
                    )

        if "o" in st:

            @pl.loop(1, D)
            def _(k):
                r = rem(row + k, D)
                remote(acc.at[g, rows(T * r, T), :], got.at[g, row], o_send.at[g], o_recv.at[g], r, col).start()

            pltpu.make_async_copy(acc.at[g, rows(T * row, T), :], got.at[g, row], o_recv.at[g]).start()

    mine = alpha_ref[pl.ds(4 * row + div(col, 4), 1), :]
    mine = pltpu.roll(mine, rem(128 - T * rem(col, 4), 128), 1)
    mine = jnp.transpose(jnp.broadcast_to(mine, (128, 128)))[0:T]

    if "f" in st:

        @pl.when(full)
        def _():
            wait_bytes(at.at[pl.ds(0, T * 15 + T // 2), :], own_send)

    if "x" in st:
        wait_bytes(sbuf.at[row, pl.ds(0, B - Q), :], x_send)
    for c in s_sent + j_sent:
        c.wait_send()
    lane = lax.broadcasted_iota(jnp.int32, (1, 128), 1)
    for g in range(2):
        if "o" in st:
            wait_bytes(got.at[g], o_recv.at[g])
        for b in range(D):
            for k in range(B // 128):
                part = got[g, 15 - b if g else b, :, 128 * (k // 2) : 128 * (k // 2 + 1)]
                start = B * b + 128 * k
                tile = slice(start, start + 128)
                if g == 0:
                    total = -mine * alpha_ref[start // 128 : start // 128 + 1, :]
                else:
                    total = out_ref[:, tile]
                for m in range(4):
                    shift = (Q * m - 64 * (k % 2) + Q * g) % 128
                    moved = pltpu.roll(part, shift, 1) if shift else part
                    total += jnp.where(div(lane, Q) == 2 * m + g, moved, 0.0)
                out_ref[:, tile] = total
    if "o" in st:
        for g in range(2):
            wait_bytes(acc.at[g, pl.ds(0, B - T), :], o_send.at[g])


def solution(mesh, st="fxsjco"):
    def body(a, alpha):
        B = a.shape[0]
        T, H, R = B // D, B // 2, (B // D) * 17
        dma = pltpu.SemaphoreType.DMA
        return pl.pallas_call(
            functools.partial(kernel, st, B),
            out_shape=jax.ShapeDtypeStruct((T, B * D), jnp.float32),
            in_specs=[pl.BlockSpec(memory_space=pltpu.HBM), pl.BlockSpec(memory_space=pltpu.VMEM)],
            out_specs=pl.BlockSpec(memory_space=pltpu.VMEM),
            scratch_shapes=[
                pltpu.VMEM((B, B), jnp.bfloat16),
                pltpu.VMEM((B, B), jnp.bfloat16),
                pltpu.VMEM((D, R, H), jnp.bfloat16),
                pltpu.VMEM((D, R, H), jnp.bfloat16),
                pltpu.VMEM((2, B, H), jnp.float32),
                pltpu.VMEM((2, D, T, H), jnp.float32),
                dma,
                dma((30,)),
                dma((2, D)),
                dma,
                dma,
                dma,
                dma((15 * SUB,)),
                dma((D, SUB)),
                dma((2,)),
                dma((2,)),
            ],
            compiler_params=pltpu.CompilerParams(
                collective_id=0, has_side_effects=True, vmem_limit_bytes=VM
            ),
        )(a, alpha.reshape(B * D // 128, 128))

    return jax.shard_map(
        body, mesh=mesh, in_specs=(P("row", "col"), P(None)), out_specs=P(("row", "col"), None), check_vma=False
    )
```

time: 91.4 us -> 80.7 us (0.88); the launches traced: 91.2 us -> 79.6 us
  Pallas kernels: 88.3 us -> 76.8 us
  other arithmetic: 1.12 us -> 0 us
  local copies, waits for them, and re-layouts: 1.8 us -> 2.77 us
    pallas_call x1, Pallas kernels: 88.3 us -> 76.8 us  [body(): pl.pallas_call(functools.partial(kernel, st, B), out_shape=jax.ShapeDtype...]
    unnamed x4 -> x5, local copies, waits for them, and re-layouts: 1.04 us -> 2.77 us
    sub x1 -> x0, other arithmetic: 1.12 us -> none  [body(): return g - mine[:, None] * alpha[None, :]]
where the time goes in v3:
time: 80.7 us; the launch traced here: 79.6 us
  Pallas kernels  76.8 us (95%)
  local copies, waits for them, and re-layouts  2.77 us (3%)
    pallas_call x1, Pallas kernels, body(): pl.pallas_call(functools.partial(kernel, st, B), out_shape=jax.ShapeDtype...  76.8 us
    unnamed x5, local copies, waits for them, and re-layouts  2.77 us

profile of v3, /device:TPU:25, one launch (start us, length us, event | category | flops | bytes accessed | tf_op | source)
XLA Modules:
  0.0 79.6 jit_solution(8063924520020347036)
XLA Ops:
  0.0 0.0 copy-start
  0.0 1.0 %copy-done = bf16[512,512]{1,0:T(8,128)(2,1)S(1)} copy-done((bf16[512,512]{1,0:T(8,128)(2,1)S(1)}, bf16[512,512]{1,0:T(8,128)(2,1)}, u32[]{:S(2)}) %copy-start) | copy-done | bytes 524312
  1.0 0.0 copy-start.1
  1.0 0.8 copy-done.1
  1.8 76.8 %shard_map.28 = f32[32,8192]{1,0:T(8,128)S(1)} custom-call(bf16[512,512]{1,0:T(8,128)(2,1)S(1)} %copy-done, f32[64,128]{1,0:T(8,128)S(1)} %bitcast.1), custom_call_target="tpu_custom_call" | custom-call | tf_op jit(solution)/shard_map/pallas_call | solution.py:277
  78.6 1.0 %copy.4 = f32[32,8192]{1,0:T(8,128)} copy(f32[32,8192]{1,0:T(8,128)S(1)} %shard_map.28) | data formatting | bytes 2097152
Async XLA Ops:
  0.0 1.0 %copy-start = (bf16[512,512]{1,0:T(8,128)(2,1)S(1)}, bf16[512,512]{1,0:T(8,128)(2,1)}, u32[]{:S(2)}) copy-start(bf16[512,512]{1,0:T(8,128)(2,1)} %a_hbm.1) | copy-start | bytes 1572868
  1.0 0.8 copy-start.1

commit v4 on v3

--- a/solution.py
+++ b/solution.py
@@ -9,7 +9,8 @@
 
 MESH = pl.DeviceIdType.MESH
 D = 16
-SUB = 2
+CUTS = (0, 4, 8, 12, 17)
+SUB = len(CUTS) - 1
 VM = 40 * 1024 * 1024
 
 
@@ -19,6 +20,10 @@
 
 def rem(a, b):
     return lax.rem(a, jnp.int32(b))
+
+
+def fold(c):
+    return c + div(c, 8) * (15 - 2 * c)
 
 
 def kernel(
@@ -37,6 +42,7 @@
     s_send,
     s_recv,
     own_send,
+    own_recv,
     x_send,
     x_recv,
     j_send,
@@ -45,12 +51,13 @@
     o_recv,
 ):
     T, H, R = B // D, B // 2, (B // D) * 17
-    Q, half, sub = T // 2, R // 2, R // SUB
+    Q, half = T // 2, R // 2
     row, col = lax.axis_index("row"), lax.axis_index("col")
     x, y, core = div(row, 4), rem(row, 4), rem(col, 2)
     sign = 1 - 2 * core
     mirror = 15 - row
     full = row >= col
+    m = fold(row)
 
     def rows(start, n):
         return pl.ds(pl.multiple_of(start, Q), n)
@@ -97,38 +104,49 @@
             @pl.loop(0, D)
             def _(k):
                 i = far_first(k)
-                remote(at.at[rows(T * i, T), pl.ds(H, H)], high, own_send, s_recv.at[0, mirror], mirror, i).start()
+                remote(at.at[rows(T * i, T), pl.ds(H, H)], high, own_send, own_recv.at[16 - row + col], mirror, i).start()
 
             @pl.loop(0, D - 1)
             def _(k):
                 i = far_first(k)
-                remote(at.at[rows(T * i, T), pl.ds(0, H)], low, own_send, s_recv.at[0, row], row, i).start()
-
-            pltpu.make_async_copy(at.at[rows(piece, T), pl.ds(0, H)], low, s_recv.at[0, row]).start()
-
-        wait_bytes(sbuf.at[row], s_recv.at[0, row])
+                remote(at.at[rows(T * i, T), pl.ds(0, H)], low, own_send, own_recv.at[col], row, i).start()
+
+            pltpu.make_async_copy(at.at[rows(piece, T), pl.ds(0, H)], low, own_recv.at[col]).start()
+
 
     if "x" in st:
-        here = row * T
-
-        def pair(p):
-            gx = div(row + 16 - p, 16)
-            gy = div(row + 1 + p, 16)
-            base = T * (row + 1)
-            first = gx * (T * p) + (1 - gx) * (base + T * (15 - p) + Q)
-            second = gy * (T * (15 - p) + Q) + (1 - gy) * (base + T * p)
-            return first, second
-
-        @pl.loop(1, D)
+
+        def pass_on(c, place, q, second):
+            wait_bytes(sbuf.at[row, rows(T * place, T), :], own_recv.at[place])
+            late = div(c, 8)
+            start = T * (late * (q - c) + (1 - late) * (16 + c - q)) + Q * second
+            dst = jbuf.at[col, rows(start, Q), :]
+            for n, r in enumerate((c, 15 - c)):
+                src = sbuf.at[row, rows(T * place + Q * n, Q), :]
+
+                @pl.when(r == row)
+                def _(src=src):
+                    pltpu.make_async_copy(src, dst, x_recv).start()
+
+                @pl.when(r != row)
+                def _(src=src, r=r):
+                    remote(src, dst, x_send, x_recv, r, col).start()
+
+        @pl.loop(0, D)
         def _(k):
-            p = rem(row + k, D)
-            for n, start in enumerate(pair(p)):
-                remote(sbuf.at[row, rows(start, Q), :], jbuf.at[col, rows(here + Q * n, Q), :], x_send, x_recv, p, col).start()
-
-        remote(sbuf.at[row, pl.ds(B, Q), :], jbuf.at[col, pl.ds(B + Q, Q), :], x_send, x_recv, mirror, col).start()
-        for n, start in enumerate(pair(row)):
-            pltpu.make_async_copy(sbuf.at[row, rows(start, Q), :], jbuf.at[col, rows(here + Q * n, Q), :], x_recv).start()
-        pltpu.make_async_copy(sbuf.at[row, pl.ds(B + Q, Q), :], jbuf.at[col, pl.ds(B, Q), :], x_recv).start()
+            c = far_first(k)
+
+            @pl.when(c <= mirror)
+            def _():
+                pass_on(c, row + 1 + c, mirror, 1)
+
+        @pl.loop(0, D)
+        def _(k):
+            c = far_first(k)
+
+            @pl.when(c <= row)
+            def _():
+                pass_on(c, c, row, 0)
 
     s_sent = []
 
@@ -169,7 +187,7 @@
     def j_pass(t, u, targets, own=False):
         if "j" not in st:
             return
-        part = jbuf.at[t, pl.ds(u * sub, sub), :]
+        part = jbuf.at[t, pl.ds(T * CUTS[u], T * (CUTS[u + 1] - CUTS[u])), :]
         if not own:
             wait_bytes(part, j_recv.at[t, u])
         for c in targets:
@@ -191,38 +209,29 @@
         j_pass(col, u, (other,), True)
     when = [(5.0, s_step, (1, 0)), (5.1, s_step, (-1, 0)), (8.0, s_step, (0, 1)), (9.5, s_step, (2, 0)),
             (12.5, s_step, (1, 1)), (12.6, s_step, (-1, 1)), (17.0, s_step, (2, 1))]
-    for d in range(1, 5):
+    for d in range(1, 4):
         for u in range(SUB):
             when.append((4 + 5 * d + 6 / SUB * u, j_step, (d, u)))
     for _, step, args in sorted(when, key=lambda e: e[0]):
         step(*args)
     for d1, d2 in [(0, -1), (0, 2), (1, -1), (-1, -1), (1, 2), (-1, 2), (2, -1), (2, 2)]:
         s_step(d1, d2)
-    for d in range(8):
-        for u in range(SUB):
+
+    def j_rest(u):
+        for d in range(8):
             j_pass(rem(other + 2 * d, D), u, ())
 
     def right(start):
-        return jbuf[:, start, :].reshape(H, H)
+        return jbuf[:, rows(start, Q), :].reshape(H, H)
 
     def times(lhs, rhs):
         return lax.dot_general(lhs, rhs, (((1,), (1,)), ((), ())), preferred_element_type=jnp.float32)
 
-    for g in range(2):
-        first_block = mirror if g else row
-        if "c" in st:
-            acc[g] = jnp.zeros_like(acc[g])
-            for q in range(D):
-                n = T * (q + 1)
-
-                @pl.when(q >= first_block)
-                def _(q=q, n=n, g=g):
-                    at_end = 1 - div(q - first_block + 15, 16)
-                    start = (1 - at_end) * (T * (15 - q) + Q * (1 - g)) + at_end * (B + Q * (1 - g))
-                    acc[g, 0:n, :] += times(sbuf[q, 0:n, :], right(pl.ds(T * q + Q * g, Q))) + times(
-                        sbuf[15 - q, R - n : R, :], right(rows(start, Q))
-                    )
-
+    def add(g, q, start):
+        n = T * (q + 1)
+        acc[g, 0:n, :] += times(sbuf[q, 0:n, :], right(start)) + times(sbuf[15 - q, R - n : R, :], right(start + Q))
+
+    def send(g):
         if "o" in st:
 
             @pl.loop(1, D)
@@ -232,6 +241,39 @@
 
             pltpu.make_async_copy(acc.at[g, rows(T * row, T), :], got.at[g, row], o_recv.at[g]).start()
 
+    acc[...] = jnp.zeros_like(acc)
+    for u in (0, 1):
+        j_step(4, u)
+    for u in (0, 1):
+        j_rest(u)
+    if "c" in st:
+        for q in reversed(range(8, D)):
+
+            @pl.when(q >= 15 - m)
+            def _(q=q):
+                add(0, q, T * (q - 15 + m))
+
+    send(0)
+    for u in (2, 3):
+        j_step(4, u)
+    j_rest(2)
+    if "c" in st:
+        for q in reversed(range(5, D)):
+
+            @pl.when(q >= m + 5)
+            def _(q=q):
+                add(1, q, T * (16 + m - q))
+
+    j_rest(3)
+    if "c" in st:
+        for q in reversed(range(12)):
+
+            @pl.when(jnp.logical_and(q >= m, q < m + 5))
+            def _(q=q):
+                add(1, q, T * (16 + m - q))
+
+    send(1)
+
     mine = alpha_ref[pl.ds(4 * row + div(col, 4), 1), :]
     mine = pltpu.roll(mine, rem(128 - T * rem(col, 4), 128), 1)
     mine = jnp.transpose(jnp.broadcast_to(mine, (128, 128)))[0:T]
@@ -246,24 +288,26 @@
         wait_bytes(sbuf.at[row, pl.ds(0, B - Q), :], x_send)
     for c in s_sent + j_sent:
         c.wait_send()
-    lane = lax.broadcasted_iota(jnp.int32, (1, 128), 1)
+    lane = lax.broadcasted_iota(jnp.int32, (T, 128), 1)
+    early = rem(lane, T) < Q
+    group = [div(lane, T) == m for m in range(4)]
     for g in range(2):
         if "o" in st:
             wait_bytes(got.at[g], o_recv.at[g])
-        for b in range(D):
+        for b in range(8) if g else range(8, D):
             for k in range(B // 128):
-                part = got[g, 15 - b if g else b, :, 128 * (k // 2) : 128 * (k // 2 + 1)]
                 start = B * b + 128 * k
-                tile = slice(start, start + 128)
-                if g == 0:
-                    total = -mine * alpha_ref[start // 128 : start // 128 + 1, :]
-                else:
-                    total = out_ref[:, tile]
-                for m in range(4):
-                    shift = (Q * m - 64 * (k % 2) + Q * g) % 128
-                    moved = pltpu.roll(part, shift, 1) if shift else part
-                    total += jnp.where(div(lane, Q) == 2 * m + g, moved, 0.0)
-                out_ref[:, tile] = total
+                wide = []
+                for n in range(2):
+                    part = got[g, 15 - b if n else b, :, 128 * (k // 2) : 128 * (k // 2 + 1)]
+                    for i in range(4):
+                        shift = (Q * i - 64 * (k % 2) + Q * n) % 128
+                        moved = pltpu.roll(part, shift, 1) if shift else part
+                        total = jnp.where(group[i], moved, total) if i else moved
+                    wide.append(total)
+                out_ref[:, start : start + 128] = (
+                    jnp.where(early, *wide) - mine * alpha_ref[start // 128 : start // 128 + 1, :]
+                )
     if "o" in st:
         for g in range(2):
             wait_bytes(acc.at[g, pl.ds(0, B - T), :], o_send.at[g])
@@ -290,6 +334,7 @@
                 dma((30,)),
                 dma((2, D)),
                 dma,
+                dma((D + 1,)),
                 dma,
                 dma,
                 dma((15 * SUB,)),

time: 80.7 us -> 76.8 us (0.952)
  Pallas kernels: 76.8 us -> 73.6 us
    pallas_call x1, Pallas kernels: 76.8 us -> 73.6 us  [body(): pl.pallas_call(functools.partial(kernel, st, B), out_shape=jax.ShapeDtype...]
where the time goes in v4:
time: 76.8 us; the launch traced here: 76.4 us
  Pallas kernels  73.6 us (96%)
  local copies, waits for them, and re-layouts  2.77 us (4%)
    pallas_call x1, Pallas kernels, body(): pl.pallas_call(functools.partial(kernel, st, B), out_shape=jax.ShapeDtype...  73.6 us
    unnamed x5, local copies, waits for them, and re-layouts  2.77 us

profile of v4, /device:TPU:25, one launch (start us, length us, event | category | flops | bytes accessed | tf_op | source)
XLA Modules:
  0.0 76.4 jit_solution(1848640878022197511)
XLA Ops:
  0.0 0.0 copy-start
  0.0 1.0 %copy-done = bf16[512,512]{1,0:T(8,128)(2,1)S(1)} copy-done((bf16[512,512]{1,0:T(8,128)(2,1)S(1)}, bf16[512,512]{1,0:T(8,128)(2,1)}, u32[]{:S(2)}) %copy-start) | copy-done | bytes 524312
  1.0 0.0 copy-start.1
  1.0 0.8 copy-done.1
  1.8 73.6 %shard_map.28 = f32[32,8192]{1,0:T(8,128)S(1)} custom-call(bf16[512,512]{1,0:T(8,128)(2,1)S(1)} %copy-done, f32[64,128]{1,0:T(8,128)S(1)} %bitcast.1), custom_call_target="tpu_custom_call" | custom-call | tf_op jit(solution)/shard_map/pallas_call | solution.py:321
  75.4 1.0 %copy.4 = f32[32,8192]{1,0:T(8,128)} copy(f32[32,8192]{1,0:T(8,128)S(1)} %shard_map.28) | data formatting | bytes 2097152
Async XLA Ops:
  0.0 1.0 %copy-start = (bf16[512,512]{1,0:T(8,128)(2,1)S(1)}, bf16[512,512]{1,0:T(8,128)(2,1)}, u32[]{:S(2)}) copy-start(bf16[512,512]{1,0:T(8,128)(2,1)} %a_hbm.1) | copy-start | bytes 1572868
  1.0 0.8 copy-start.1

commit v5 on v4

--- a/solution.py
+++ b/solution.py
@@ -9,7 +9,8 @@
 
 MESH = pl.DeviceIdType.MESH
 D = 16
-CUTS = (0, 4, 8, 12, 17)
+REACH = 819.0
+CUTS = (0, 8, 14, 17)
 SUB = len(CUTS) - 1
 VM = 40 * 1024 * 1024
 
@@ -24,6 +25,10 @@
 
 def fold(c):
     return c + div(c, 8) * (15 - 2 * c)
+
+
+def place_of(c):
+    return 8 * div(c, 8) + 2 * rem(c, 4) + div(rem(c, 8), 4)
 
 
 def kernel(
@@ -37,7 +42,11 @@
     sbuf,
     jbuf,
     acc,
+    code,
+    unit,
     got,
+    units,
+    ready,
     a_sem,
     s_send,
     s_recv,
@@ -49,6 +58,8 @@
     j_recv,
     o_send,
     o_recv,
+    u_send,
+    u_recv,
 ):
     T, H, R = B // D, B // 2, (B // D) * 17
     Q, half = T // 2, R // 2
@@ -78,10 +89,6 @@
     load = pltpu.make_async_copy(a_hbm, a_ref, a_sem)
     load.start()
 
-    @pl.loop(0, D)
-    def _(k):
-        greet(mirror, rem(col + k, D))
-
     @pl.loop(1, D)
     def _(k):
         greet(row, rem(col + k, D))
@@ -89,15 +96,20 @@
 
     load.wait()
     at[...] = jnp.transpose(a_ref[...])
-    pl.semaphore_wait(barrier, 46)
+    pl.semaphore_wait(barrier, 30)
+    pl.semaphore_signal(ready, inc=1, device_id=(mirror, col), device_id_type=MESH)
 
     def far_first(k):
         return rem(col + 24 + (1 - 2 * rem(k, 2)) * div(k + 1, 2), D)
 
+    if "f" not in st:
+        pl.semaphore_wait(ready, 1)
     if "f" in st:
         piece = T * col
         low = sbuf.at[row, rows(piece, T), :]
         high = sbuf.at[mirror, rows(T * (16 - row) + piece, T), :]
+
+        pl.semaphore_wait(ready, 1)
 
         @pl.when(full)
         def _():
@@ -106,6 +118,8 @@
                 i = far_first(k)
                 remote(at.at[rows(T * i, T), pl.ds(H, H)], high, own_send, own_recv.at[16 - row + col], mirror, i).start()
 
+        @pl.when(full)
+        def _():
             @pl.loop(0, D - 1)
             def _(k):
                 i = far_first(k)
@@ -113,24 +127,25 @@
 
             pltpu.make_async_copy(at.at[rows(piece, T), pl.ds(0, H)], low, own_recv.at[col]).start()
 
-
     if "x" in st:
 
         def pass_on(c, place, q, second):
             wait_bytes(sbuf.at[row, rows(T * place, T), :], own_recv.at[place])
             late = div(c, 8)
-            start = T * (late * (q - c) + (1 - late) * (16 + c - q)) + Q * second
-            dst = jbuf.at[col, rows(start, Q), :]
+            unit_at = late * (q - c) + (1 - late) * (16 + c - q)
+            start = T * unit_at + Q * second
+            arrived = x_recv.at[sum(div(unit_at + 32 - cut, 32) for cut in CUTS[1:-1])]
+            dst = jbuf.at[place_of(col), rows(start, Q), :]
             for n, r in enumerate((c, 15 - c)):
                 src = sbuf.at[row, rows(T * place + Q * n, Q), :]
 
                 @pl.when(r == row)
                 def _(src=src):
-                    pltpu.make_async_copy(src, dst, x_recv).start()
+                    pltpu.make_async_copy(src, dst, arrived).start()
 
                 @pl.when(r != row)
                 def _(src=src, r=r):
-                    remote(src, dst, x_send, x_recv, r, col).start()
+                    remote(src, dst, x_send, arrived, r, col).start()
 
         @pl.loop(0, D)
         def _(k):
@@ -184,14 +199,17 @@
     def z_at(d):
         return rem(col + 2 * sign * d + 32, D)
 
+    def group_of(t, u):
+        return jbuf.at[place_of(t), pl.ds(T * CUTS[u], T * (CUTS[u + 1] - CUTS[u])), :]
+
     def j_pass(t, u, targets, own=False):
         if "j" not in st:
             return
-        part = jbuf.at[t, pl.ds(T * CUTS[u], T * (CUTS[u + 1] - CUTS[u])), :]
+        part = group_of(t, u)
         if not own:
-            wait_bytes(part, j_recv.at[t, u])
+            wait_bytes(part, j_recv.at[place_of(t), u])
         for c in targets:
-            cp = remote(part, part, j_send.at[len(j_sent)], j_recv.at[t, u], row, c)
+            cp = remote(part, part, j_send.at[len(j_sent)], j_recv.at[place_of(t), u], row, c)
             cp.start()
             j_sent.append(cp)
 
@@ -201,9 +219,9 @@
             j_pass(z_at(d), u, ((z_at(-1),) if d < 3 else ()) + (other,))
 
     s_step(0, 0)
-    if "x" in st:
-        wait_bytes(jbuf.at[col], x_recv)
     for u in range(SUB):
+        if "x" in st:
+            wait_bytes(group_of(col, u), x_recv.at[u])
         j_pass(col, u, (z_at(1), z_at(-1)), True)
     for u in range(SUB):
         j_pass(col, u, (other,), True)
@@ -232,19 +250,29 @@
         acc[g, 0:n, :] += times(sbuf[q, 0:n, :], right(start)) + times(sbuf[15 - q, R - n : R, :], right(start + Q))
 
     def send(g):
-        if "o" in st:
-
-            @pl.loop(1, D)
-            def _(k):
-                r = rem(row + k, D)
-                remote(acc.at[g, rows(T * r, T), :], got.at[g, row], o_send.at[g], o_recv.at[g], r, col).start()
-
-            pltpu.make_async_copy(acc.at[g, rows(T * row, T), :], got.at[g, row], o_recv.at[g]).start()
+        if "o" not in st:
+            return
+        top = jnp.maximum(jnp.max(jnp.abs(acc[g]), keepdims=True), 1e-30)
+        one = acc[g] * (REACH / top)
+        two = one * one
+        four = two * two
+        code[g] = (four * four * four * one).astype(jnp.bfloat16)
+        unit[g] = jnp.broadcast_to(top * (1.0 / REACH), (8, 128))
+
+        @pl.loop(1, D)
+        def _(k):
+            r = rem(row + k, D)
+            remote(code.at[g, rows(T * r, T), :], got.at[g, row], o_send.at[g], o_recv.at[g], r, col).start()
+            remote(unit.at[g], units.at[g, row], u_send.at[g], u_recv.at[g], r, col).start()
+
+        pltpu.make_async_copy(code.at[g, rows(T * row, T), :], got.at[g, row], o_recv.at[g]).start()
+        pltpu.make_async_copy(unit.at[g], units.at[g, row], u_recv.at[g]).start()
 
     acc[...] = jnp.zeros_like(acc)
-    for u in (0, 1):
+    light = CUTS.index(8)
+    for u in range(light):
         j_step(4, u)
-    for u in (0, 1):
+    for u in range(light):
         j_rest(u)
     if "c" in st:
         for q in reversed(range(8, D)):
@@ -254,24 +282,20 @@
                 add(0, q, T * (q - 15 + m))
 
     send(0)
-    for u in (2, 3):
+    high = D
+    for u in range(light, SUB):
         j_step(4, u)
-    j_rest(2)
-    if "c" in st:
-        for q in reversed(range(5, D)):
-
-            @pl.when(q >= m + 5)
-            def _(q=q):
-                add(1, q, T * (16 + m - q))
-
-    j_rest(3)
-    if "c" in st:
-        for q in reversed(range(12)):
-
-            @pl.when(jnp.logical_and(q >= m, q < m + 5))
-            def _(q=q):
-                add(1, q, T * (16 + m - q))
-
+    for u in range(light, SUB):
+        j_rest(u)
+        low = m + 17 - CUTS[u + 1]
+        if "c" in st:
+            for q in reversed(range(17 - CUTS[u + 1], min(D, 24 - CUTS[u]) if u > light else D)):
+
+                @pl.when(jnp.logical_and(q >= low, q < high))
+                def _(q=q):
+                    add(1, q, T * (16 + m - q))
+
+        high = low
     send(1)
 
     mine = alpha_ref[pl.ds(4 * row + div(col, 4), 1), :]
@@ -290,27 +314,30 @@
         c.wait_send()
     lane = lax.broadcasted_iota(jnp.int32, (T, 128), 1)
     early = rem(lane, T) < Q
-    group = [div(lane, T) == m for m in range(4)]
     for g in range(2):
         if "o" in st:
             wait_bytes(got.at[g], o_recv.at[g])
+            wait_bytes(units.at[g], u_recv.at[g])
+
+        def decode(r, tile, g=g):
+            value = got[g, r, :, tile].astype(jnp.float32)
+            size = jnp.exp(jnp.log(jnp.abs(value)) * (1.0 / 13.0)) * units[g, r, 0:1, :]
+            return jnp.where(value < 0.0, -size, size)
+
         for b in range(8) if g else range(8, D):
-            for k in range(B // 128):
-                start = B * b + 128 * k
-                wide = []
-                for n in range(2):
-                    part = got[g, 15 - b if n else b, :, 128 * (k // 2) : 128 * (k // 2 + 1)]
-                    for i in range(4):
-                        shift = (Q * i - 64 * (k % 2) + Q * n) % 128
-                        moved = pltpu.roll(part, shift, 1) if shift else part
-                        total = jnp.where(group[i], moved, total) if i else moved
-                    wide.append(total)
-                out_ref[:, start : start + 128] = (
-                    jnp.where(early, *wide) - mine * alpha_ref[start // 128 : start // 128 + 1, :]
-                )
+            for k in range(H // 128):
+                tile = slice(128 * k, 128 * (k + 1))
+                near, far = decode(b, tile), decode(15 - b, tile)
+                start = B * b + 256 * k
+                for n, value in enumerate(
+                    (jnp.where(early, near, pltpu.roll(far, Q, 1)), jnp.where(early, pltpu.roll(near, 128 - Q, 1), far))
+                ):
+                    first = start + 128 * n
+                    out_ref[:, first : first + 128] = value - mine * alpha_ref[first // 128 : first // 128 + 1, :]
     if "o" in st:
         for g in range(2):
-            wait_bytes(acc.at[g, pl.ds(0, B - T), :], o_send.at[g])
+            wait_bytes(code.at[g, pl.ds(0, B - T), :], o_send.at[g])
+            wait_bytes(units.at[g, pl.ds(0, D - 1)], u_send.at[g])
 
 
 def solution(mesh, st="fxsjco"):
@@ -329,16 +356,22 @@
                 pltpu.VMEM((D, R, H), jnp.bfloat16),
                 pltpu.VMEM((D, R, H), jnp.bfloat16),
                 pltpu.VMEM((2, B, H), jnp.float32),
-                pltpu.VMEM((2, D, T, H), jnp.float32),
+                pltpu.VMEM((2, B, H), jnp.bfloat16),
+                pltpu.VMEM((2, 8, 128), jnp.float32),
+                pltpu.VMEM((2, D, T, H), jnp.bfloat16),
+                pltpu.VMEM((2, D, 8, 128), jnp.float32),
+                pltpu.SemaphoreType.REGULAR,
                 dma,
                 dma((30,)),
                 dma((2, D)),
                 dma,
                 dma((D + 1,)),
                 dma,
-                dma,
+                dma((SUB,)),
                 dma((15 * SUB,)),
                 dma((D, SUB)),
+                dma((2,)),
+                dma((2,)),
                 dma((2,)),
                 dma((2,)),
             ],

time: 76.8 us -> 72.5 us (0.944); the launches traced: 76.4 us -> 71.1 us
  Pallas kernels: 73.6 us -> 68.3 us
    pallas_call x1, Pallas kernels: 73.6 us -> 68.3 us  [body(): pl.pallas_call(functools.partial(kernel, st, B), out_shape=jax.ShapeDtype...]
where the time goes in v5:
time: 72.5 us; the launch traced here: 71.1 us
  Pallas kernels  68.3 us (94%)
  local copies, waits for them, and re-layouts  2.77 us (4%)
    pallas_call x1, Pallas kernels, body(): pl.pallas_call(functools.partial(kernel, st, B), out_shape=jax.ShapeDtype...  68.3 us
    unnamed x5, local copies, waits for them, and re-layouts  2.77 us

profile of v5, /device:TPU:25, one launch (start us, length us, event | category | flops | bytes accessed | tf_op | source)
XLA Modules:
  0.0 71.1 jit_solution(16356918765068677650)
XLA Ops:
  0.0 0.0 copy-start
  0.0 1.0 %copy-done = bf16[512,512]{1,0:T(8,128)(2,1)S(1)} copy-done((bf16[512,512]{1,0:T(8,128)(2,1)S(1)}, bf16[512,512]{1,0:T(8,128)(2,1)}, u32[]{:S(2)}) %copy-start) | copy-done | bytes 524312
  1.0 0.0 copy-start.1
  1.0 0.8 %copy-done.1 = f32[8192]{0:T(1024)S(1)} copy-done((f32[8192]{0:T(1024)S(1)}, f32[8192]{0:T(1024)}, u32[]{:S(2)}) %copy-start.1) | copy-done | bytes 32792
  1.8 68.3 %shard_map.28 = f32[32,8192]{1,0:T(8,128)S(1)} custom-call(bf16[512,512]{1,0:T(8,128)(2,1)S(1)} %copy-done, f32[64,128]{1,0:T(8,128)S(1)} %bitcast.1), custom_call_target="tpu_custom_call" | custom-call | tf_op jit(solution)/shard_map/pallas_call | solution.py:348
  70.2 1.0 %copy.4 = f32[32,8192]{1,0:T(8,128)} copy(f32[32,8192]{1,0:T(8,128)S(1)} %shard_map.28) | data formatting | bytes 2097152
Async XLA Ops:
  0.0 1.0 %copy-start = (bf16[512,512]{1,0:T(8,128)(2,1)S(1)}, bf16[512,512]{1,0:T(8,128)(2,1)}, u32[]{:S(2)}) copy-start(bf16[512,512]{1,0:T(8,128)(2,1)} %a_hbm.1) | copy-start | bytes 1572868
  1.0 0.8 %copy-start.1 = (f32[8192]{0:T(1024)S(1)}, f32[8192]{0:T(1024)}, u32[]{:S(2)}) copy-start(f32[8192]{0:T(1024)} %param.3) | copy-start | bytes 98308

commit v6 on v5

--- a/solution.py
+++ b/solution.py
@@ -147,21 +147,13 @@
                 def _(src=src, r=r):
                     remote(src, dst, x_send, arrived, r, col).start()
 
-        @pl.loop(0, D)
-        def _(k):
-            c = far_first(k)
-
-            @pl.when(c <= mirror)
-            def _():
-                pass_on(c, row + 1 + c, mirror, 1)
-
-        @pl.loop(0, D)
-        def _(k):
-            c = far_first(k)
-
-            @pl.when(c <= row)
-            def _():
-                pass_on(c, c, row, 0)
+        @pl.loop(0, 16 - row)
+        def _(c):
+            pass_on(c, row + 1 + c, mirror, 1)
+
+        @pl.loop(0, row + 1)
+        def _(c):
+            pass_on(c, c, row, 0)
 
     s_sent = []
 
@@ -229,7 +221,7 @@
             (12.5, s_step, (1, 1)), (12.6, s_step, (-1, 1)), (17.0, s_step, (2, 1))]
     for d in range(1, 4):
         for u in range(SUB):
-            when.append((4 + 5 * d + 6 / SUB * u, j_step, (d, u)))
+            when.append((2 + 5 * d + u, j_step, (d, u)))
     for _, step, args in sorted(when, key=lambda e: e[0]):
         step(*args)
     for d1, d2 in [(0, -1), (0, 2), (1, -1), (-1, -1), (1, 2), (-1, 2), (2, -1), (2, 2)]:
@@ -274,28 +266,23 @@
         j_step(4, u)
     for u in range(light):
         j_rest(u)
-    if "c" in st:
-        for q in reversed(range(8, D)):
-
-            @pl.when(q >= 15 - m)
-            def _(q=q):
-                add(0, q, T * (q - 15 + m))
-
+    def sums(g, lo, hi):
+        for block in range(8) if "c" in st else ():
+
+            @pl.when(m == block)
+            def _(block=block):
+                for q in reversed(range(15 - block if g == 0 else block, D)):
+                    place = q - 15 + block if g == 0 else 16 + block - q
+                    if lo <= place < hi:
+                        add(g, q, T * place)
+
+    sums(0, 0, 8)
     send(0)
-    high = D
     for u in range(light, SUB):
         j_step(4, u)
     for u in range(light, SUB):
         j_rest(u)
-        low = m + 17 - CUTS[u + 1]
-        if "c" in st:
-            for q in reversed(range(17 - CUTS[u + 1], min(D, 24 - CUTS[u]) if u > light else D)):
-
-                @pl.when(jnp.logical_and(q >= low, q < high))
-                def _(q=q):
-                    add(1, q, T * (16 + m - q))
-
-        high = low
+        sums(1, 0 if u == light else CUTS[u], CUTS[u + 1])
     send(1)
 
     mine = alpha_ref[pl.ds(4 * row + div(col, 4), 1), :]

time: 72.5 us -> 69.5 us (0.959)
  Pallas kernels: 68.3 us -> 65.5 us
    pallas_call x1, Pallas kernels: 68.3 us -> 65.5 us  [body(): pl.pallas_call(functools.partial(kernel, st, B), out_shape=jax.ShapeDtype...]
where the time goes in v6:
time: 69.5 us; the launch traced here: 68.3 us
  Pallas kernels  65.5 us (94%)
  local copies, waits for them, and re-layouts  2.77 us (4%)
    pallas_call x1, Pallas kernels, body(): pl.pallas_call(functools.partial(kernel, st, B), out_shape=jax.ShapeDtype...  65.5 us
    unnamed x5, local copies, waits for them, and re-layouts  2.77 us

profile of v6, /device:TPU:25, one launch (start us, length us, event | category | flops | bytes accessed | tf_op | source)
XLA Modules:
  0.0 68.3 jit_solution(10773740601652302542)
XLA Ops:
  0.0 0.0 copy-start
  0.0 1.0 %copy-done = bf16[512,512]{1,0:T(8,128)(2,1)S(1)} copy-done((bf16[512,512]{1,0:T(8,128)(2,1)S(1)}, bf16[512,512]{1,0:T(8,128)(2,1)}, u32[]{:S(2)}) %copy-start) | copy-done | bytes 524312
  1.0 0.0 copy-start.1
  1.0 0.8 %copy-done.1 = f32[8192]{0:T(1024)S(1)} copy-done((f32[8192]{0:T(1024)S(1)}, f32[8192]{0:T(1024)}, u32[]{:S(2)}) %copy-start.1) | copy-done | bytes 32792
  1.8 65.5 %shard_map.28 = f32[32,8192]{1,0:T(8,128)S(1)} custom-call(bf16[512,512]{1,0:T(8,128)(2,1)S(1)} %copy-done, f32[64,128]{1,0:T(8,128)S(1)} %bitcast.1), custom_call_target="tpu_custom_call" | custom-call | tf_op jit(solution)/shard_map/pallas_call | solution.py:335
  67.4 1.0 %copy.4 = f32[32,8192]{1,0:T(8,128)} copy(f32[32,8192]{1,0:T(8,128)S(1)} %shard_map.28) | data formatting | bytes 2097152
Async XLA Ops:
  0.0 1.0 %copy-start = (bf16[512,512]{1,0:T(8,128)(2,1)S(1)}, bf16[512,512]{1,0:T(8,128)(2,1)}, u32[]{:S(2)}) copy-start(bf16[512,512]{1,0:T(8,128)(2,1)} %a_hbm.1) | copy-start | bytes 1572868
  1.0 0.8 %copy-start.1 = (f32[8192]{0:T(1024)S(1)}, f32[8192]{0:T(1024)}, u32[]{:S(2)}) copy-start(f32[8192]{0:T(1024)} %param.3) | copy-start | bytes 98308

commit v7 on v6

--- a/solution.py
+++ b/solution.py
@@ -10,7 +10,7 @@
 MESH = pl.DeviceIdType.MESH
 D = 16
 REACH = 819.0
-CUTS = (0, 8, 14, 17)
+CUTS = (0, 8, 12, 17)
 SUB = len(CUTS) - 1
 VM = 40 * 1024 * 1024
 
@@ -32,12 +32,10 @@
 
 
 def kernel(
-    st,
     B,
-    a_hbm,
+    a_ref,
     alpha_ref,
     out_ref,
-    a_ref,
     at,
     sbuf,
     jbuf,
@@ -47,7 +45,6 @@
     got,
     units,
     ready,
-    a_sem,
     s_send,
     s_recv,
     own_send,
@@ -86,74 +83,67 @@
     def greet(r, c):
         pl.semaphore_signal(barrier, inc=1, device_id=(r, c), device_id_type=MESH)
 
-    load = pltpu.make_async_copy(a_hbm, a_ref, a_sem)
-    load.start()
-
     @pl.loop(1, D)
     def _(k):
         greet(row, rem(col + k, D))
         greet(rem(row + k, D), col)
 
-    load.wait()
     at[...] = jnp.transpose(a_ref[...])
+    acc[...] = jnp.zeros_like(acc)
     pl.semaphore_wait(barrier, 30)
     pl.semaphore_signal(ready, inc=1, device_id=(mirror, col), device_id_type=MESH)
 
     def far_first(k):
         return rem(col + 24 + (1 - 2 * rem(k, 2)) * div(k + 1, 2), D)
 
-    if "f" not in st:
-        pl.semaphore_wait(ready, 1)
-    if "f" in st:
-        piece = T * col
-        low = sbuf.at[row, rows(piece, T), :]
-        high = sbuf.at[mirror, rows(T * (16 - row) + piece, T), :]
-
-        pl.semaphore_wait(ready, 1)
-
-        @pl.when(full)
-        def _():
-            @pl.loop(0, D)
-            def _(k):
-                i = far_first(k)
-                remote(at.at[rows(T * i, T), pl.ds(H, H)], high, own_send, own_recv.at[16 - row + col], mirror, i).start()
-
-        @pl.when(full)
-        def _():
-            @pl.loop(0, D - 1)
-            def _(k):
-                i = far_first(k)
-                remote(at.at[rows(T * i, T), pl.ds(0, H)], low, own_send, own_recv.at[col], row, i).start()
-
-            pltpu.make_async_copy(at.at[rows(piece, T), pl.ds(0, H)], low, own_recv.at[col]).start()
-
-    if "x" in st:
-
-        def pass_on(c, place, q, second):
-            wait_bytes(sbuf.at[row, rows(T * place, T), :], own_recv.at[place])
-            late = div(c, 8)
-            unit_at = late * (q - c) + (1 - late) * (16 + c - q)
-            start = T * unit_at + Q * second
-            arrived = x_recv.at[sum(div(unit_at + 32 - cut, 32) for cut in CUTS[1:-1])]
-            dst = jbuf.at[place_of(col), rows(start, Q), :]
-            for n, r in enumerate((c, 15 - c)):
-                src = sbuf.at[row, rows(T * place + Q * n, Q), :]
-
-                @pl.when(r == row)
-                def _(src=src):
-                    pltpu.make_async_copy(src, dst, arrived).start()
-
-                @pl.when(r != row)
-                def _(src=src, r=r):
-                    remote(src, dst, x_send, arrived, r, col).start()
-
-        @pl.loop(0, 16 - row)
-        def _(c):
-            pass_on(c, row + 1 + c, mirror, 1)
-
-        @pl.loop(0, row + 1)
-        def _(c):
-            pass_on(c, c, row, 0)
+    piece = T * col
+    low = sbuf.at[row, rows(piece, T), :]
+    high = sbuf.at[mirror, rows(T * (16 - row) + piece, T), :]
+
+    pl.semaphore_wait(ready, 1)
+
+    @pl.when(full)
+    def _():
+        @pl.loop(0, D)
+        def _(k):
+            i = far_first(k)
+            remote(at.at[rows(T * i, T), pl.ds(H, H)], high, own_send, own_recv.at[16 - row + col], mirror, i).start()
+
+    @pl.when(full)
+    def _():
+        @pl.loop(0, D - 1)
+        def _(k):
+            i = far_first(k)
+            remote(at.at[rows(T * i, T), pl.ds(0, H)], low, own_send, own_recv.at[col], row, i).start()
+
+        pltpu.make_async_copy(at.at[rows(piece, T), pl.ds(0, H)], low, own_recv.at[col]).start()
+
+
+    def pass_on(c, place, q, second):
+        wait_bytes(sbuf.at[row, rows(T * place, T), :], own_recv.at[place])
+        late = div(c, 8)
+        unit_at = late * (q - c) + (1 - late) * (16 + c - q)
+        start = T * unit_at + Q * second
+        arrived = x_recv.at[sum(div(unit_at + 32 - cut, 32) for cut in CUTS[1:-1])]
+        dst = jbuf.at[place_of(col), rows(start, Q), :]
+        for n, r in enumerate((c, 15 - c)):
+            src = sbuf.at[row, rows(T * place + Q * n, Q), :]
+
+            @pl.when(r == row)
+            def _(src=src):
+                pltpu.make_async_copy(src, dst, arrived).start()
+
+            @pl.when(r != row)
+            def _(src=src, r=r):
+                remote(src, dst, x_send, arrived, r, col).start()
+
+    @pl.loop(0, 16 - row)
+    def _(c):
+        pass_on(c, row + 1 + c, mirror, 1)
+
+    @pl.loop(0, row + 1)
+    def _(c):
+        pass_on(c, c, row, 0)
 
     s_sent = []
 
@@ -167,8 +157,6 @@
         s_sent.append(c)
 
     def s_step(d1, d2):
-        if "s" not in st:
-            return
         for h in range(2):
             sg = sign if h == 0 else -sign
             turn = (lambda p, s: (p, s)) if h == 0 else (lambda p, s: (s, p))
@@ -195,8 +183,6 @@
         return jbuf.at[place_of(t), pl.ds(T * CUTS[u], T * (CUTS[u + 1] - CUTS[u])), :]
 
     def j_pass(t, u, targets, own=False):
-        if "j" not in st:
-            return
         part = group_of(t, u)
         if not own:
             wait_bytes(part, j_recv.at[place_of(t), u])
@@ -212,8 +198,7 @@
 
     s_step(0, 0)
     for u in range(SUB):
-        if "x" in st:
-            wait_bytes(group_of(col, u), x_recv.at[u])
+        wait_bytes(group_of(col, u), x_recv.at[u])
         j_pass(col, u, (z_at(1), z_at(-1)), True)
     for u in range(SUB):
         j_pass(col, u, (other,), True)
@@ -242,8 +227,6 @@
         acc[g, 0:n, :] += times(sbuf[q, 0:n, :], right(start)) + times(sbuf[15 - q, R - n : R, :], right(start + Q))
 
     def send(g):
-        if "o" not in st:
-            return
         top = jnp.maximum(jnp.max(jnp.abs(acc[g]), keepdims=True), 1e-30)
         one = acc[g] * (REACH / top)
         two = one * one
@@ -260,14 +243,13 @@
         pltpu.make_async_copy(code.at[g, rows(T * row, T), :], got.at[g, row], o_recv.at[g]).start()
         pltpu.make_async_copy(unit.at[g], units.at[g, row], u_recv.at[g]).start()
 
-    acc[...] = jnp.zeros_like(acc)
     light = CUTS.index(8)
     for u in range(light):
         j_step(4, u)
     for u in range(light):
         j_rest(u)
     def sums(g, lo, hi):
-        for block in range(8) if "c" in st else ():
+        for block in range(8):
 
             @pl.when(m == block)
             def _(block=block):
@@ -289,26 +271,23 @@
     mine = pltpu.roll(mine, rem(128 - T * rem(col, 4), 128), 1)
     mine = jnp.transpose(jnp.broadcast_to(mine, (128, 128)))[0:T]
 
-    if "f" in st:
-
-        @pl.when(full)
-        def _():
-            wait_bytes(at.at[pl.ds(0, T * 15 + T // 2), :], own_send)
-
-    if "x" in st:
-        wait_bytes(sbuf.at[row, pl.ds(0, B - Q), :], x_send)
+
+    @pl.when(full)
+    def _():
+        wait_bytes(at.at[pl.ds(0, T * 15 + T // 2), :], own_send)
+
+    wait_bytes(sbuf.at[row, pl.ds(0, B - Q), :], x_send)
     for c in s_sent + j_sent:
         c.wait_send()
     lane = lax.broadcasted_iota(jnp.int32, (T, 128), 1)
     early = rem(lane, T) < Q
     for g in range(2):
-        if "o" in st:
-            wait_bytes(got.at[g], o_recv.at[g])
-            wait_bytes(units.at[g], u_recv.at[g])
+        wait_bytes(got.at[g], o_recv.at[g])
+        wait_bytes(units.at[g], u_recv.at[g])
 
         def decode(r, tile, g=g):
             value = got[g, r, :, tile].astype(jnp.float32)
-            size = jnp.exp(jnp.log(jnp.abs(value)) * (1.0 / 13.0)) * units[g, r, 0:1, :]
+            size = jnp.exp2(jnp.log(jnp.abs(value)) * (1.4426950408889634 / 13.0)) * units[g, r, 0:1, :]
             return jnp.where(value < 0.0, -size, size)
 
         for b in range(8) if g else range(8, D):
@@ -321,24 +300,22 @@
                 ):
                     first = start + 128 * n
                     out_ref[:, first : first + 128] = value - mine * alpha_ref[first // 128 : first // 128 + 1, :]
-    if "o" in st:
-        for g in range(2):
-            wait_bytes(code.at[g, pl.ds(0, B - T), :], o_send.at[g])
-            wait_bytes(units.at[g, pl.ds(0, D - 1)], u_send.at[g])
-
-
-def solution(mesh, st="fxsjco"):
+    for g in range(2):
+        wait_bytes(code.at[g, pl.ds(0, B - T), :], o_send.at[g])
+        wait_bytes(units.at[g, pl.ds(0, D - 1)], u_send.at[g])
+
+
+def solution(mesh):
     def body(a, alpha):
         B = a.shape[0]
         T, H, R = B // D, B // 2, (B // D) * 17
         dma = pltpu.SemaphoreType.DMA
         return pl.pallas_call(
-            functools.partial(kernel, st, B),
+            functools.partial(kernel, B),
             out_shape=jax.ShapeDtypeStruct((T, B * D), jnp.float32),
-            in_specs=[pl.BlockSpec(memory_space=pltpu.HBM), pl.BlockSpec(memory_space=pltpu.VMEM)],
+            in_specs=[pl.BlockSpec(memory_space=pltpu.VMEM)] * 2,
             out_specs=pl.BlockSpec(memory_space=pltpu.VMEM),
             scratch_shapes=[
-                pltpu.VMEM((B, B), jnp.bfloat16),
                 pltpu.VMEM((B, B), jnp.bfloat16),
                 pltpu.VMEM((D, R, H), jnp.bfloat16),
                 pltpu.VMEM((D, R, H), jnp.bfloat16),
@@ -348,7 +325,6 @@
                 pltpu.VMEM((2, D, T, H), jnp.bfloat16),
                 pltpu.VMEM((2, D, 8, 128), jnp.float32),
                 pltpu.SemaphoreType.REGULAR,
-                dma,
                 dma((30,)),
                 dma((2, D)),
                 dma,

time: 69.5 us -> 69.2 us (level)
  no operation moved by 1% of the time
where the time goes in v7:
time: 69.2 us; the launch traced here: 68.1 us
  Pallas kernels  65.3 us (94%)
  local copies, waits for them, and re-layouts  2.77 us (4%)
    pallas_call x1, Pallas kernels, body(): pl.pallas_call(functools.partial(kernel, B), out_shape=jax.ShapeDtypeStru...  65.3 us
    unnamed x5, local copies, waits for them, and re-layouts  2.77 us

profile of v7, /device:TPU:25, one launch (start us, length us, event | category | flops | bytes accessed | tf_op | source)
XLA Modules:
  0.0 68.1 jit_solution(15784762212930571421)
XLA Ops:
  0.0 0.0 copy-start
  0.0 1.0 %copy-done = bf16[512,512]{1,0:T(8,128)(2,1)S(1)} copy-done((bf16[512,512]{1,0:T(8,128)(2,1)S(1)}, bf16[512,512]{1,0:T(8,128)(2,1)}, u32[]{:S(2)}) %copy-start) | copy-done | bytes 524312
  1.0 0.0 copy-start.1
  1.0 0.8 %copy-done.1 = f32[8192]{0:T(1024)S(1)} copy-done((f32[8192]{0:T(1024)S(1)}, f32[8192]{0:T(1024)}, u32[]{:S(2)}) %copy-start.1) | copy-done | bytes 32792
  1.8 65.3 %shard_map.28 = f32[32,8192]{1,0:T(8,128)S(1)} custom-call(bf16[512,512]{1,0:T(8,128)(2,1)S(1)} %copy-done, f32[64,128]{1,0:T(8,128)S(1)} %bitcast.1), custom_call_target="tpu_custom_call" | custom-call | tf_op jit(solution)/shard_map/pallas_call | solution.py:313
  67.2 1.0 %copy.4 = f32[32,8192]{1,0:T(8,128)} copy(f32[32,8192]{1,0:T(8,128)S(1)} %shard_map.28) | data formatting | bytes 2097152
Async XLA Ops:
  0.0 1.0 %copy-start = (bf16[512,512]{1,0:T(8,128)(2,1)S(1)}, bf16[512,512]{1,0:T(8,128)(2,1)}, u32[]{:S(2)}) copy-start(bf16[512,512]{1,0:T(8,128)(2,1)} %a_ref.1) | copy-start | bytes 1572868
  1.0 0.8 %copy-start.1 = (f32[8192]{0:T(1024)S(1)}, f32[8192]{0:T(1024)}, u32[]{:S(2)}) copy-start(f32[8192]{0:T(1024)} %param.3) | copy-start | bytes 98308

commit v8 on v7

--- a/solution.py
+++ b/solution.py
@@ -83,7 +83,7 @@
     def greet(r, c):
         pl.semaphore_signal(barrier, inc=1, device_id=(r, c), device_id_type=MESH)
 
-    @pl.loop(1, D)
+    @pl.loop(1, D, unroll=True)
     def _(k):
         greet(row, rem(col + k, D))
         greet(rem(row + k, D), col)
@@ -104,14 +104,14 @@
 
     @pl.when(full)
     def _():
-        @pl.loop(0, D)
+        @pl.loop(0, D, unroll=True)
         def _(k):
             i = far_first(k)
             remote(at.at[rows(T * i, T), pl.ds(H, H)], high, own_send, own_recv.at[16 - row + col], mirror, i).start()
 
     @pl.when(full)
     def _():
-        @pl.loop(0, D - 1)
+        @pl.loop(0, D - 1, unroll=True)
         def _(k):
             i = far_first(k)
             remote(at.at[rows(T * i, T), pl.ds(0, H)], low, own_send, own_recv.at[col], row, i).start()
@@ -234,7 +234,7 @@
         code[g] = (four * four * four * one).astype(jnp.bfloat16)
         unit[g] = jnp.broadcast_to(top * (1.0 / REACH), (8, 128))
 
-        @pl.loop(1, D)
+        @pl.loop(1, D, unroll=True)
         def _(k):
             r = rem(row + k, D)
             remote(code.at[g, rows(T * r, T), :], got.at[g, row], o_send.at[g], o_recv.at[g], r, col).start()

time: 69.2 us -> 69.2 us (level)
  no operation moved by 1% of the time
where the time goes in v8:
time: 69.2 us; the launch traced here: 68.2 us
  Pallas kernels  65.4 us (95%)
  local copies, waits for them, and re-layouts  2.77 us (4%)
    pallas_call x1, Pallas kernels, body(): pl.pallas_call(functools.partial(kernel, B), out_shape=jax.ShapeDtypeStru...  65.4 us
    unnamed x5, local copies, waits for them, and re-layouts  2.77 us

profile of v8, /device:TPU:25, one launch (start us, length us, event | category | flops | bytes accessed | tf_op | source)
XLA Modules:
  0.0 68.2 jit_solution(15221405697849849868)
XLA Ops:
  0.0 0.0 copy-start
  0.0 1.0 %copy-done = bf16[512,512]{1,0:T(8,128)(2,1)S(1)} copy-done((bf16[512,512]{1,0:T(8,128)(2,1)S(1)}, bf16[512,512]{1,0:T(8,128)(2,1)}, u32[]{:S(2)}) %copy-start) | copy-done | bytes 524312
  1.0 0.0 copy-start.1
  1.0 0.8 %copy-done.1 = f32[8192]{0:T(1024)S(1)} copy-done((f32[8192]{0:T(1024)S(1)}, f32[8192]{0:T(1024)}, u32[]{:S(2)}) %copy-start.1) | copy-done | bytes 32792
  1.8 65.4 %shard_map.28 = f32[32,8192]{1,0:T(8,128)S(1)} custom-call(bf16[512,512]{1,0:T(8,128)(2,1)S(1)} %copy-done, f32[64,128]{1,0:T(8,128)S(1)} %bitcast.1), custom_call_target="tpu_custom_call" | custom-call | tf_op jit(solution)/shard_map/pallas_call | solution.py:313
  67.2 1.0 %copy.4 = f32[32,8192]{1,0:T(8,128)} copy(f32[32,8192]{1,0:T(8,128)S(1)} %shard_map.28) | data formatting | bytes 2097152
Async XLA Ops:
  0.0 1.0 %copy-start = (bf16[512,512]{1,0:T(8,128)(2,1)S(1)}, bf16[512,512]{1,0:T(8,128)(2,1)}, u32[]{:S(2)}) copy-start(bf16[512,512]{1,0:T(8,128)(2,1)} %a_ref.1) | copy-start | bytes 1572868
  1.0 0.8 %copy-start.1 = (f32[8192]{0:T(1024)S(1)}, f32[8192]{0:T(1024)}, u32[]{:S(2)}) copy-start(f32[8192]{0:T(1024)} %param.3) | copy-start | bytes 98308
